TPU v7x, 32 devices: a whole 2x2x4 slice. The times are simulated.
32 devices in a mesh: dp: 8 (over y, x, core), tensor: 4 (over z).
Axes of the slice: x: 2, y: 2, z: 4, core: 2. Of those that a mesh axis runs over, the one named last changes fastest.
Arguments:
- grad_tokens: bfloat16 [1536, 2048], P('dp', 'tensor'), may hold values from -6 to 6
- hidden_input: bfloat16 [2048, 5120], P('dp', 'tensor'), may hold values from -6 to 6
- output_weight: bfloat16 [5120, 2048], P(None, 'tensor'), may hold values from -0.078125 to 0.078125
- image_tokens: int32 [8, 8], replicated, may hold values from 0 to 192, as said below
- moved_images: int32 [8], replicated, may hold values from 0 to 7, as said below
Outputs:
- input_grad: bfloat16 [2048, 5120], P('dp', 'tensor')
- weight_grad: float32 [5120, 2048], P('dp', 'tensor')
- bias_grad: float32 [2048], P('tensor')
Inputs may be any that keep to these rules, and one draw needn't show every extreme that they name: `image_tokens`: row s lists the merged tokens of sample s's images in order: 1 to 8 positive entries, then zeros; each row sums to 192. `moved_images`: entry s is less than the number of images of sample s; those trailing images hold at most 64 merged tokens together, exactly 64 for some sample in every draw. They are encoded by owner s + 1 (owner 0 after the last).
All inputs are finite; a program needn't handle non-finite values.
Results may differ from a plain program's by a relative error of at most 0.014.
Values may be sent and summed in bfloat16 or wider, within the bound.
A program may use at most 64 MiB of HBM per device.

v0:
```python
import jax
import jax.numpy as jnp
from jax import lax
from jax.sharding import PartitionSpec as P

root_half = 0.7071067811865476
inv_root_tau = 0.3989422804014327


def from_behind(value, axis, steps):
    count = lax.axis_size(axis)
    pairs = [(source, (source + steps) % count) for source in range(count)]
    return lax.ppermute(value, axis, pairs)


def gelu_parts(values):
    normal_cdf = 0.5 * (1.0 + jax.scipy.special.erf(values * root_half))
    density = jnp.exp(-0.5 * values * values) * inv_root_tau
    return (values * normal_cdf, normal_cdf + values * density)


def kept_lengths(image_tokens, moved_images):
    present = jnp.sum((image_tokens > 0).astype(jnp.int32), axis=1)
    slot_ids = jnp.arange(image_tokens.shape[1], dtype=jnp.int32)
    kept_mask = slot_ids[None, :] < (present - moved_images)[:, None]
    return jnp.sum(jnp.where(kept_mask, image_tokens, 0), axis=1)


def per_device(grad_tokens, hidden_input, output_weight, image_tokens, moved_images):
    dp_count = lax.axis_size("dp")
    dp_index = lax.axis_index("dp")
    tok_rows = grad_tokens.shape[0]
    buffer_rows = hidden_input.shape[0]
    tail_count = buffer_rows - tok_rows
    keep_len = kept_lengths(image_tokens, moved_images)
    own_keep = jnp.sum(jnp.where(jnp.arange(dp_count, dtype=jnp.int32) == dp_index, keep_len, 0))
    positions = jnp.arange(tok_rows, dtype=jnp.int32)[:, None]
    zero_value = jnp.zeros((), jnp.bfloat16)
    kept_rows = jnp.where(positions < own_keep, grad_tokens, zero_value)
    moving = jnp.where(
        positions[tok_rows - tail_count :] >= own_keep,
        grad_tokens[tok_rows - tail_count :],
        zero_value,
    )
    arrived = from_behind(moving, "dp", 1)
    grad_rows = jnp.concatenate([kept_rows, arrived], axis=0)
    bias_grad = lax.psum(jnp.sum(grad_tokens.astype(jnp.float32), axis=0), "dp")
    activation, slopes = gelu_parts(hidden_input.astype(jnp.float32))
    partials = lax.dot_general(
        grad_rows, output_weight, (((1,), (1,)), ((), ())), preferred_element_type=jnp.float32
    )
    grad_hidden = lax.psum_scatter(
        partials.astype(jnp.bfloat16), "tensor", scatter_dimension=1, tiled=True
    ).astype(jnp.float32)
    input_grad = (grad_hidden * slopes).astype(jnp.bfloat16)
    gathered_input = lax.all_gather(hidden_input, "tensor", axis=1, tiled=True)
    full_act = gelu_parts(gathered_input.astype(jnp.float32))[0].astype(jnp.bfloat16)
    hidden_width = full_act.shape[1]
    rows_each = (hidden_width + 8 * dp_count - 1) // (8 * dp_count) * 8
    padded = jnp.pad(full_act, ((0, 0), (0, rows_each * dp_count - hidden_width)))
    weight_grad = lax.psum_scatter(
        lax.dot_general(
            padded, grad_rows, (((0,), (0,)), ((), ())), preferred_element_type=jnp.float32
        ),
        "dp",
        scatter_dimension=0,
        tiled=True,
    )
    return (input_grad, weight_grad, bias_grad)


def solution(mesh):
    return jax.shard_map(
        per_device,
        mesh=mesh,
        in_specs=(P("dp", "tensor"), P("dp", "tensor"), P(None, "tensor"), P(), P()),
        out_specs=(P("dp", "tensor"), P("dp", "tensor"), P("tensor")),
        check_vma=False,
    )
```

profile of v0, /device:TPU:0, one launch (start us, length us, event | category | flops | bytes accessed | tf_op | source)
XLA Modules:
  0.0 212.5 jit_solution(6390169746239598268)
XLA Ops:
  7.2 0.0 all-gather.2.cloned.1.call-start
  7.2 0.7 all-gather.2.cloned.1.call-update
  7.9 0.0 reduce-scatter.3.cloned.1.call-start
  7.9 0.8 convert_reduce_fusion.1
  8.8 0.7 sub.3
  9.4 0.9 select_reduce_fusion
  10.3 0.6 fusion.17
  10.9 0.7 compare_bitcast_fusion
  11.6 0.9 slice_select_fusion
  12.5 0.5 collective-permute-start
  13.0 0.6 iota_compare_fusion.1
  13.7 1.0 broadcast_select_fusion
  14.7 3.1 %collective-permute-done = bf16[64,512]{1,0:T(8,128)(2,1)S(1)} collective-permute-done((bf16[64,512]{1,0:T(8,128)(2,1)S(1)}, bf16[64,512]{1,0:T(8,128)(2,1)S(1)}, u32[]{:S(2)}, u32[]{:S(2)}) %collective-permute-start) | collective-permute-done | bytes 65568 | tf_op jit(solution)/shard_map/ppermute | solution.py:13
  17.9 5.9 %convolution_convert_fusion = bf16[256,5120]{1,0:T(8,128)(2,1)} fusion(bf16[5120,512]{1,0:T(8,128)(2,1)} %param.7, bf16[64,512]{1,0:T(8,128)(2,1)S(1)} %collective-permute-done, bf16[192,512]{1,0:T(8,128)(2,1)S(1)} %broadcast_select_fusion), kind=kOutput, calls=%fused_computation.2 | convolution fusion | flops 1344012288 | bytes 8126464 | tf_op jit(solution)/shard_map/dot_general | solution.py:49
  23.8 0.0 reduce-scatter.3.cloned.1.call-update
  23.8 0.0 reduce-scatter.5.cloned.1.call-start
  23.8 43.2 %all-gather.2.cloned.1.call-done = bf16[256,5120]{1,0:T(8,128)(2,1)} async-done(((bf16[256,1280]{1,0:T(8,128)(2,1)}), bf16[256,5120]{1,0:T(8,128)(2,1)}) %all-gather.2.cloned.1.call-update) | async-done | bytes 2621456 | tf_op jit(solution)/shard_map/all_gather | solution.py:56
  67.0 7.3 %fusion.4 = f32[5120,512]{1,0:T(8,128)} fusion(bf16[256,5120]{1,0:T(8,128)(2,1)} %all-gather.2.cloned.1.call-done, bf16[64,512]{1,0:T(8,128)(2,1)S(1)} %collective-permute-done, bf16[192,512]{1,0:T(8,128)(2,1)S(1)} %broadcast_select_fusion), kind=kOutput, calls=%fused_computation.7 | convolution fusion | flops 1350565888 | bytes 13369344 | tf_op jit(solution)/shard_map/dot_general | solution.py:62
  74.4 0.0 copy-start.1
  74.4 0.0 copy-start
  74.4 0.0 reduce-scatter.5.cloned.1.call-update
  74.4 0.9 copy-done.1
  75.3 14.6 %psum.7 = f32[512]{0:T(512)} all-reduce(f32[512]{0:T(512)S(1)} %convert_reduce_fusion), channel_id=1, replica_groups=mesh['dp'=8,'tensor'=4] {'dp'}, use_global_device_ids=true, to_apply=%region_6.7 | all-reduce | flops 512 | bytes 4096 | tf_op jit(solution)/shard_map/psum | solution.py:47
  89.9 30.5 %reduce-scatter.3.cloned.1.call-done = bf16[256,1280]{1,0:T(8,128)(2,1)} async-done(((bf16[256,5120]{1,0:T(8,128)(2,1)}), bf16[256,1280]{1,0:T(8,128)(2,1)}) %reduce-scatter.3.cloned.1.call-update) | async-done | bytes 655376 | tf_op jit(solution)/shard_map/reduce_scatter | solution.py:52
  120.4 0.0 copy-done
  120.4 2.5 %fusion.16 = bf16[256,1280]{1,0:T(8,128)(2,1)} fusion(bf16[256,1280]{1,0:T(8,128)(2,1)S(1)} %copy-done, bf16[256,1280]{1,0:T(8,128)(2,1)} %reduce-scatter.3.cloned.1.call-done), kind=kLoop, calls=%fused_computation.22 | loop fusion | flops 3932160 | bytes 1966080 | tf_op jit(solution)/shard_map/convert_element_type | solution.py:55
  122.9 83.1 %reduce-scatter.5.cloned.1.call-done = f32[640,512]{1,0:T(8,128)} async-done(((f32[5120,512]{1,0:T(8,128)}), f32[640,512]{1,0:T(8,128)}) %reduce-scatter.5.cloned.1.call-update) | async-done | bytes 1310736 | tf_op jit(solution)/shard_map/reduce_scatter | solution.py:61
  (1 shorter events, 0.0 us)
Async XLA Ops:
  7.2 59.9 %all-gather.2.cloned.1.call-start = ((), (), s32[]{:S(2)}) async-start(), calls=%async_computation.3 | async-start | bytes 3276800 | tf_op jit(solution)/shard_map/all_gather | solution.py:56
  7.9 112.5 %reduce-scatter.3.cloned.1.call-start = ((), (), s32[]{:S(2)}) async-start(), calls=%async_computation.2 | async-start | bytes 3276800 | tf_op jit(solution)/shard_map/reduce_scatter | solution.py:52
  12.5 5.4 %collective-permute-start = (bf16[64,512]{1,0:T(8,128)(2,1)S(1)}, bf16[64,512]{1,0:T(8,128)(2,1)S(1)}, u32[]{:S(2)}, u32[]{:S(2)}) collective-permute-start(bf16[64,512]{1,0:T(8,128)(2,1)S(1)} %slice_select_fusion), channel_id=1, source_target_pairs={{0,4},{4,8},{8,12},{12,16},{16,20},{20,24},{24,28},{28,0},{1,5},{5... | collective-permute-start | bytes 196616 | tf_op jit(solution)/shard_map/ppermute | solution.py:13
  23.8 182.2 %reduce-scatter.5.cloned.1.call-start = ((), (), s32[]{:S(2)}) async-start(), calls=%async_computation.4 | async-start | bytes 11796480 | tf_op jit(solution)/shard_map/reduce_scatter | solution.py:61
  74.4 0.9 copy-start.1
  74.4 46.0 %copy-start = (bf16[256,1280]{1,0:T(8,128)(2,1)S(1)}, bf16[256,1280]{1,0:T(8,128)(2,1)}, u32[]{:S(2)}) copy-start(bf16[256,1280]{1,0:T(8,128)(2,1)} %param.6) | copy-start | bytes 1966084
Sparse Core Ops, SparseCore 0:
  9.5 57.4 all-gather.1
  69.3 51.0 reduce-scatter.2
  124.5 81.4 reduce-scatter.4
where the time goes:
time: 213 us
  waiting for transfers between devices  161 us (76%)
  blocking collectives  14.6 us (7%)
  between operations  13.8 us (6%)
  matrix products  13.2 us (6%)
  other arithmetic  8.8 us (4%)
    reduce_scatter x1, waiting for transfers between devices, per_device(): lax.psum_scatter(lax.dot_general(padded, grad_rows, (((0,), (0,)), ((), (...  83.1 us
    all_gather x1, waiting for transfers between devices, per_device(): gathered_input = lax.all_gather(hidden_input, 'tensor', axis=1, tiled=True)  43.2 us
    reduce_scatter x1, waiting for transfers between devices, per_device(): lax.psum_scatter(partials.astype(jnp.bfloat16), 'tensor', scatter_dimensi...  30.5 us
    psum x1, blocking collectives, per_device(): bias_grad = lax.psum(jnp.sum(grad_tokens.astype(jnp.float32), axis=0), 'dp')  14.6 us
    dot_general x1, matrix products, per_device(): lax.dot_general(padded, grad_rows, (((0,), (0,)), ((), ())), preferred_el...  7.31 us
    dot_general x1, matrix products, per_device(): lax.dot_general(grad_rows, output_weight, (((1,), (1,)), ((), ())), prefe...  5.9 us
  transfers between devices with their start and end apart: 4, of which 4 were waited for; matrix products, arithmetic and copies ran while one was open for 10% of the time, Pallas kernels for 0%

commit v1 on v0

--- a/solution.py
+++ b/solution.py
@@ -53,7 +53,14 @@
         partials.astype(jnp.bfloat16), "tensor", scatter_dimension=1, tiled=True
     ).astype(jnp.float32)
     input_grad = (grad_hidden * slopes).astype(jnp.bfloat16)
-    gathered_input = lax.all_gather(hidden_input, "tensor", axis=1, tiled=True)
+    ring = [hidden_input]
+    for hop in range(3):
+        ring.append(lax.ppermute(ring[-1], "tensor", [(dev, (dev + 1) % 4) for dev in range(4)]))
+    gathered_input = jnp.roll(
+        jnp.concatenate(ring[::-1], axis=1),
+        (lax.axis_index("tensor") + 1) * ring[0].shape[1],
+        axis=1,
+    )
     full_act = gelu_parts(gathered_input.astype(jnp.float32))[0].astype(jnp.bfloat16)
     hidden_width = full_act.shape[1]
     rows_each = (hidden_width + 8 * dp_count - 1) // (8 * dp_count) * 8

time: 213 us -> 206 us (0.967)
  waiting for transfers between devices: 161 us -> 138 us
  starting transfers between devices: 0.66 us -> 19.2 us
  blocking collectives: 14.6 us -> 12.4 us
    ppermute x0 -> x3, waiting for transfers between devices: none -> 69.9 us  [per_device(): lax.ppermute(ring[-1], 'tensor', [(dev, (dev + 1) % 4) for dev in range(4)])]
    all_gather x1 -> x0, waiting for transfers between devices: 43.2 us -> none  [per_device(): gathered_input = lax.all_gather(hidden_input, 'tensor', axis=1, tiled=True)]
    reduce_scatter x1, waiting for transfers between devices: 30.5 us -> 0.01 us  [per_device(): lax.psum_scatter(partials.astype(jnp.bfloat16), 'tensor', scatter_dimensi...]
    ppermute x0 -> x3, starting transfers between devices: none -> 18.6 us  [per_device(): lax.ppermute(ring[-1], 'tensor', [(dev, (dev + 1) % 4) for dev in range(4)])]
    reduce_scatter x1, waiting for transfers between devices: 83.1 us -> 64.7 us  [per_device(): lax.psum_scatter(lax.dot_general(padded, grad_rows, (((0,), (0,)), ((), (...]
    psum x1, blocking collectives: 14.6 us -> 12.4 us  [per_device(): bias_grad = lax.psum(jnp.sum(grad_tokens.astype(jnp.float32), axis=0), 'dp')]
  transfers between devices with their start and end apart: 4 -> 6, of which waited for: 4 -> 5; matrix products, arithmetic and copies ran while one was open for 10% -> 5% of each run, Pallas kernels for 0% -> 0%
where the time goes in v1:
time: 206 us; the launch traced here: 205 us
  waiting for transfers between devices  138 us (67%)
  starting transfers between devices  19.2 us (9%)
  between operations  14.2 us (7%)
  blocking collectives  12.4 us (6%)
  matrix products  11.6 us (6%)
  other arithmetic  8.88 us (4%)
    ppermute x3, waiting for transfers between devices, per_device(): lax.ppermute(ring[-1], 'tensor', [(dev, (dev + 1) % 4) for dev in range(4)])  69.9 us
    reduce_scatter x1, waiting for transfers between devices, per_device(): lax.psum_scatter(lax.dot_general(padded, grad_rows, (((0,), (0,)), ((), (...  64.7 us
    ppermute x3, starting transfers between devices, per_device(): lax.ppermute(ring[-1], 'tensor', [(dev, (dev + 1) % 4) for dev in range(4)])  18.6 us
    psum x1, blocking collectives, per_device(): bias_grad = lax.psum(jnp.sum(grad_tokens.astype(jnp.float32), axis=0), 'dp')  12.4 us
    dot_general x1, matrix products, per_device(): lax.dot_general(padded, grad_rows, (((0,), (0,)), ((), ())), preferred_el...  6.07 us
    dot_general x1, matrix products, per_device(): lax.dot_general(grad_rows, output_weight, (((1,), (1,)), ((), ())), prefe...  5.56 us
  transfers between devices with their start and end apart: 6, of which 5 were waited for; matrix products, arithmetic and copies ran while one was open for 5% of the time, Pallas kernels for 0%

profile of v1, /device:TPU:0, one launch (start us, length us, event | category | flops | bytes accessed | tf_op | source)
XLA Modules:
  0.0 205.5 jit_solution(14021581415114108127)
XLA Ops:
  7.2 0.0 reduce-scatter.3.cloned.1.call-start
  7.2 0.8 convert_reduce_fusion.1
  8.0 0.7 sub.7
  8.7 0.9 select_reduce_fusion
  9.5 0.6 fusion.18
  10.2 0.7 compare_bitcast_fusion
  10.8 0.9 slice_select_fusion
  11.8 0.5 collective-permute-start
  12.3 0.6 iota_compare_fusion.1
  13.0 1.0 broadcast_select_fusion
  14.0 0.0 copy-start
  14.0 3.1 %collective-permute-done = bf16[64,512]{1,0:T(8,128)(2,1)S(1)} collective-permute-done((bf16[64,512]{1,0:T(8,128)(2,1)S(1)}, bf16[64,512]{1,0:T(8,128)(2,1)S(1)}, u32[]{:S(2)}, u32[]{:S(2)}) %collective-permute-start) | collective-permute-done | bytes 65568 | tf_op jit(solution)/shard_map/ppermute | solution.py:13
  17.1 5.6 %convolution_convert_fusion = bf16[256,5120]{1,0:T(8,128)(2,1)} fusion(bf16[5120,512]{1,0:T(8,128)(2,1)} %param.7, bf16[64,512]{1,0:T(8,128)(2,1)S(1)} %collective-permute-done, bf16[192,512]{1,0:T(8,128)(2,1)S(1)} %broadcast_select_fusion), kind=kOutput, calls=%fused_computation.2 | convolution fusion | flops 1344012288 | bytes 8126464 | tf_op jit(solution)/shard_map/dot_general | solution.py:49
  22.7 0.0 reduce-scatter.3.cloned.1.call-update
  22.7 0.0 reduce-scatter.5.cloned.1.call-start
  22.8 0.0 copy-done
  22.8 2.4 %collective-permute-start.1 = (bf16[256,1280]{1,0:T(8,128)(2,1)S(1)}, bf16[256,1280]{1,0:T(8,128)(2,1)S(1)}, u32[]{:S(2)}, u32[]{:S(2)}) collective-permute-start(bf16[256,1280]{1,0:T(8,128)(2,1)S(1)} %copy-done), channel_id=1, source_target_pairs={{0,1},{1,2},{2,3},{3,0},{4,5},{5,6},{6,7},{7,4},{8,9},{9,10},{10,1... | collective-permute-start | bytes 1966088 | tf_op jit(solution)/shard_map/ppermute | solution.py:58
  25.2 24.7 %collective-permute-done.1 = bf16[256,1280]{1,0:T(8,128)(2,1)S(1)} collective-permute-done((bf16[256,1280]{1,0:T(8,128)(2,1)S(1)}, bf16[256,1280]{1,0:T(8,128)(2,1)S(1)}, u32[]{:S(2)}, u32[]{:S(2)}) %collective-permute-start.1) | collective-permute-done | bytes 655392 | tf_op jit(solution)/shard_map/ppermute | solution.py:58
  49.9 8.8 %collective-permute-start.2 = (bf16[256,1280]{1,0:T(8,128)(2,1)S(1)}, bf16[256,1280]{1,0:T(8,128)(2,1)S(1)}, u32[]{:S(2)}, u32[]{:S(2)}) collective-permute-start(bf16[256,1280]{1,0:T(8,128)(2,1)S(1)} %collective-permute-done.1), channel_id=1, source_target_pairs={{0,1},{1,2},{2,3},{3,0},{4,5},{5,6},{6,7},{7,4},{8,9},{9,10},{10,1... | collective-permute-start | bytes 1966088 | tf_op jit(solution)/shard_map/ppermute | solution.py:58
  58.7 29.4 %collective-permute-done.2 = bf16[256,1280]{1,0:T(8,128)(2,1)S(1)} collective-permute-done((bf16[256,1280]{1,0:T(8,128)(2,1)S(1)}, bf16[256,1280]{1,0:T(8,128)(2,1)S(1)}, u32[]{:S(2)}, u32[]{:S(2)}) %collective-permute-start.2) | collective-permute-done | bytes 655392 | tf_op jit(solution)/shard_map/ppermute | solution.py:58
  88.1 7.4 %collective-permute-start.3 = (bf16[256,1280]{1,0:T(8,128)(2,1)S(1)}, bf16[256,1280]{1,0:T(8,128)(2,1)S(1)}, u32[]{:S(2)}, u32[]{:S(2)}) collective-permute-start(bf16[256,1280]{1,0:T(8,128)(2,1)S(1)} %collective-permute-done.2), channel_id=1, source_target_pairs={{0,1},{1,2},{2,3},{3,0},{4,5},{5,6},{6,7},{7,4},{8,9},{9,10},{10,1... | collective-permute-start | bytes 1966088 | tf_op jit(solution)/shard_map/ppermute | solution.py:58
  95.4 15.8 %collective-permute-done.3 = bf16[256,1280]{1,0:T(8,128)(2,1)S(1)} collective-permute-done((bf16[256,1280]{1,0:T(8,128)(2,1)S(1)}, bf16[256,1280]{1,0:T(8,128)(2,1)S(1)}, u32[]{:S(2)}, u32[]{:S(2)}) %collective-permute-start.3) | collective-permute-done | bytes 655392 | tf_op jit(solution)/shard_map/ppermute | solution.py:58
  111.2 0.1 constant_dynamic-update-slice_fusion.7
  111.3 0.1 constant_dynamic-update-slice_fusion.6
  111.4 0.1 constant_dynamic-update-slice_fusion.5
  111.5 0.1 constant_dynamic-update-slice_fusion.4
  111.5 0.1 constant_dynamic-update-slice_fusion.3
  111.6 0.1 constant_dynamic-update-slice_fusion.2
  111.7 0.1 constant_dynamic-update-slice_fusion.1
  111.8 0.1 constant_dynamic-update-slice_fusion
  111.9 6.1 %fusion.4 = f32[5120,512]{1,0:T(8,128)} fusion(bf16[256,10240]{1,0:T(8,128)(2,1)S(1)} %constant_dynamic-update-slice_fusion, s32[]{:T(128)S(6)} %select_n.34, bf16[64,512]{1,0:T(8,128)(2,1)S(1)} %collective-permute-done, bf16[192,512]{1,0:T(8,128)(2,1)S(1)} %broadcast_select_fusion), kind=kOutput, calls=%fused_computation.7 | convolution fusion | flops 1350565888 | bytes 13369348 | tf_op jit(solution)/shard_map/dot_general | solution.py:69
  117.9 0.0 copy-start.1
  117.9 0.0 reduce-scatter.5.cloned.1.call-update
  118.0 0.9 copy-done.1
  118.9 12.4 %psum.7 = f32[512]{0:T(512)} all-reduce(f32[512]{0:T(512)S(1)} %convert_reduce_fusion), channel_id=1, replica_groups=mesh['dp'=8,'tensor'=4] {'dp'}, use_global_device_ids=true, to_apply=%region_6.7 | all-reduce | flops 512 | bytes 4096 | tf_op jit(solution)/shard_map/psum | solution.py:47
  131.3 0.0 reduce-scatter.3.cloned.1.call-done
  131.3 2.6 %fusion.17 = bf16[256,1280]{1,0:T(8,128)(2,1)} fusion(bf16[256,1280]{1,0:T(8,128)(2,1)S(1)} %copy-done, bf16[256,1280]{1,0:T(8,128)(2,1)} %reduce-scatter.3.cloned.1.call-done), kind=kLoop, calls=%fused_computation.23 | loop fusion | flops 3932160 | bytes 1966080 | tf_op jit(solution)/shard_map/convert_element_type | solution.py:55
  133.9 64.7 %reduce-scatter.5.cloned.1.call-done = f32[640,512]{1,0:T(8,128)} async-done(((f32[5120,512]{1,0:T(8,128)}), f32[640,512]{1,0:T(8,128)}) %reduce-scatter.5.cloned.1.call-update) | async-done | bytes 1310736 | tf_op jit(solution)/shard_map/reduce_scatter | solution.py:68
  (1 shorter events, 0.0 us)
Async XLA Ops:
  7.2 124.1 %reduce-scatter.3.cloned.1.call-start = ((), (), s32[]{:S(2)}) async-start(), calls=%async_computation.2 | async-start | bytes 3276800 | tf_op jit(solution)/shard_map/reduce_scatter | solution.py:52
  11.8 5.4 %collective-permute-start = (bf16[64,512]{1,0:T(8,128)(2,1)S(1)}, bf16[64,512]{1,0:T(8,128)(2,1)S(1)}, u32[]{:S(2)}, u32[]{:S(2)}) collective-permute-start(bf16[64,512]{1,0:T(8,128)(2,1)S(1)} %slice_select_fusion), channel_id=1, source_target_pairs={{0,4},{4,8},{8,12},{12,16},{16,20},{20,24},{24,28},{28,0},{1,5},{5... | collective-permute-start | bytes 196616 | tf_op jit(solution)/shard_map/ppermute | solution.py:13
  14.0 8.8 %copy-start = (bf16[256,1280]{1,0:T(8,128)(2,1)S(1)}, bf16[256,1280]{1,0:T(8,128)(2,1)}, u32[]{:S(2)}) copy-start(bf16[256,1280]{1,0:T(8,128)(2,1)} %param.6) | copy-start | bytes 1966084
  22.7 175.9 %reduce-scatter.5.cloned.1.call-start = ((), (), s32[]{:S(2)}) async-start(), calls=%async_computation.3 | async-start | bytes 11796480 | tf_op jit(solution)/shard_map/reduce_scatter | solution.py:68
  22.8 27.1 %collective-permute-start.1 = (bf16[256,1280]{1,0:T(8,128)(2,1)S(1)}, bf16[256,1280]{1,0:T(8,128)(2,1)S(1)}, u32[]{:S(2)}, u32[]{:S(2)}) collective-permute-start(bf16[256,1280]{1,0:T(8,128)(2,1)S(1)} %copy-done), channel_id=1, source_target_pairs={{0,1},{1,2},{2,3},{3,0},{4,5},{5,6},{6,7},{7,4},{8,9},{9,10},{10,1... | collective-permute-start | bytes 1966088 | tf_op jit(solution)/shard_map/ppermute | solution.py:58
  49.9 38.2 %collective-permute-start.2 = (bf16[256,1280]{1,0:T(8,128)(2,1)S(1)}, bf16[256,1280]{1,0:T(8,128)(2,1)S(1)}, u32[]{:S(2)}, u32[]{:S(2)}) collective-permute-start(bf16[256,1280]{1,0:T(8,128)(2,1)S(1)} %collective-permute-done.1), channel_id=1, source_target_pairs={{0,1},{1,2},{2,3},{3,0},{4,5},{5,6},{6,7},{7,4},{8,9},{9,10},{10,1... | collective-permute-start | bytes 1966088 | tf_op jit(solution)/shard_map/ppermute | solution.py:58
  88.1 23.2 %collective-permute-start.3 = (bf16[256,1280]{1,0:T(8,128)(2,1)S(1)}, bf16[256,1280]{1,0:T(8,128)(2,1)S(1)}, u32[]{:S(2)}, u32[]{:S(2)}) collective-permute-start(bf16[256,1280]{1,0:T(8,128)(2,1)S(1)} %collective-permute-done.2), channel_id=1, source_target_pairs={{0,1},{1,2},{2,3},{3,0},{4,5},{5,6},{6,7},{7,4},{8,9},{9,10},{10,1... | collective-permute-start | bytes 1966088 | tf_op jit(solution)/shard_map/ppermute | solution.py:58
  117.9 0.9 copy-start.1
Sparse Core Ops, SparseCore 0:
  22.8 77.0 reduce-scatter.2
  118.1 80.5 reduce-scatter.4
